TPU v7x, 32 devices: a whole 2x2x4 slice. The times are simulated.
32 devices in a mesh: ctx: 8 (over y, x, core), head: 4 (over z).
Axes of the slice: x: 2, y: 2, z: 4, core: 2. Of those that a mesh axis runs over, the one named last changes fastest.
Arguments:
- q_latent: bfloat16 [2048, 1536], P('ctx', 'head'), may hold values from -70 to 70
- kv_latent: bfloat16 [2048, 576], P('ctx', 'head'), may hold values from -6 to 6
- w_query: bfloat16 [1536, 12288], P(None, 'head'), may hold values from -0.15625 to 0.15625
- w_key: bfloat16 [512, 8192], P(None, 'head'), may hold values from -0.25 to 0.25
- w_value: bfloat16 [512, 8192], P(None, 'head'), may hold values from -0.25 to 0.25
- d_out: bfloat16 [2048, 8192], P('ctx', 'head'), may hold values from -6 to 6
Outputs:
- attn_out: bfloat16 [2048, 8192], P('ctx', 'head')
- grad_qlat: float32 [2048, 1536], P('ctx', 'head')
- grad_kvlat: float32 [2048, 576], P('ctx', 'head')
All inputs are finite; a program needn't handle non-finite values.
Results may differ from a plain program's by a relative error of at most 0.023.
The roundings to bfloat16 on the way count: a program that leaves them out, or rounds other values in their place, can miss the bound.
Values may be sent and summed in bfloat16 or wider, within the bound.
A program may use at most 128 MiB of HBM per device.

v0:
```python
import functools
import math

import jax
import jax.numpy as jnp
from jax import lax
from jax.experimental import pallas as pl
from jax.experimental.pallas import tpu as pltpu
from jax.sharding import PartitionSpec as P

KVL = 512
ROPE = 64
NOPE = 128
VDIM = 128
WIDTH = NOPE + ROPE
SCALE = WIDTH ** (-0.5)
F32 = jnp.float32
BF16 = jnp.bfloat16
MESH = pl.DeviceIdType.MESH


def nn(a, b):
    return jnp.dot(a, b, preferred_element_type=F32)


def nt(a, b):
    return lax.dot_general(a, b, (((1,), (1,)), ((), ())), preferred_element_type=F32)


def kernel(
    n_ctx, n_head, chunks,
    q_ref, kv_ref, do_ref, wq_hbm, wk_hbm, wv_hbm,
    out_ref, gq_ref, gkv_ref,
    wq, wk, wv, wkt, wvt, dot_t, q_in, kv_in, kv_prev, lat, lat_t, q_acc, q_t,
    keys, keys_t, values, values_t, gq_t, gk, gv, gk_sum, gv_sum, kr_sum, krope, back_out, back_in,
    rq_out, rq_right, rq_left, rkv_out, rkv_right, rkv_left, gkv_own, stage_right, stage_left,
    bias, w_sem, kv_r, kv_l, kv_recv, q_r, q_l, q_recv, p_send, p_recv,
    b_send, b_recv, rq_send, rq_rr, rq_rl, rkv_send, rkv_rr, rkv_rl,
):
    ctx = lax.axis_index("ctx")
    me = lax.axis_index("head")
    last = n_head - 1
    rows, q_cols = q_ref.shape
    part_rows = rows // chunks
    kv_cols = kv_ref.shape[0]
    heads = wk.shape[1] // NOPE
    after = {"ctx": lax.rem(ctx + 1, n_ctx)}
    before = {"ctx": lax.rem(ctx + n_ctx - 1, n_ctx)}
    right = {"head": jnp.minimum(me + 1, last)}
    left = {"head": jnp.maximum(me - 1, 0)}
    has_right = me < last
    has_left = me > 0

    loads = [
        pltpu.make_async_copy(src, dst, w_sem.at[i])
        for i, (src, dst) in enumerate(((wk_hbm, wk), (wv_hbm, wv), (wq_hbm, wq)))
    ]
    for load in loads:
        load.start()

    barrier = pltpu.get_barrier_semaphore()

    @pl.when(has_right)
    def _():
        pl.semaphore_signal(barrier, inc=1, device_id=right, device_id_type=MESH)

    @pl.when(has_left)
    def _():
        pl.semaphore_signal(barrier, inc=1, device_id=left, device_id_type=MESH)

    pl.semaphore_signal(barrier, inc=1, device_id=after, device_id_type=MESH)
    pl.semaphore_signal(barrier, inc=1, device_id=before, device_id_type=MESH)
    pl.semaphore_wait(barrier, 2 + jnp.minimum(me, 1) + jnp.minimum(last - me, 1))

    def copy_of(src, dst, send_sem, recv_sem, device):
        return pltpu.make_async_remote_copy(
            src_ref=src, dst_ref=dst, send_sem=send_sem, recv_sem=recv_sem,
            device_id=device, device_id_type=MESH,
        )

    class Gather:
        def __init__(self, own, slots, send_r, send_l, recv):
            self.own, self.slots, self.recv = own, slots, recv
            self.send_r, self.send_l = send_r, send_l

        def moves(self, t, act):
            @pl.when(has_right & (me >= t))
            def _():
                owner = me - t
                src = self.own if t == 0 else self.slots(owner)
                act(copy_of(src, self.slots(owner), self.send_r(t), self.recv(owner), right))

            @pl.when(has_left & (me + t <= last))
            def _():
                owner = me + t
                src = self.own if t == 0 else self.slots(owner)
                act(copy_of(src, self.slots(owner), self.send_l(t), self.recv(owner), left))

        def start(self, t):
            if t < last:
                self.moves(t, lambda copy: copy.start())

        def each(self, t, act):
            @pl.when(me - 1 - t >= 0)
            def _():
                act(me - 1 - t)

            @pl.when(me + 1 + t <= last)
            def _():
                act(me + 1 + t)

        def arrive(self, t, act=None):
            def wait(owner):
                slot = self.slots(owner)
                copy_of(slot, slot, self.send_r(0), self.recv(owner), right).wait_recv()
                if act is not None:
                    act(owner)

            self.each(t, wait)
            self.start(t + 1)

        def finish(self):
            for t in range(last):
                self.moves(t, lambda copy: copy.wait_send())

    def pass_on(owner, src):
        copy_of(src, kv_prev.at[owner], p_send.at[owner], p_recv.at[owner], after).start()

    kv_gather = Gather(kv_ref, lambda i: kv_in.at[i], lambda t: kv_r.at[t], lambda t: kv_l.at[t], lambda i: kv_recv.at[i])
    q_gathers = [
        Gather(
            q_ref.at[pl.ds(c * part_rows, part_rows), :],
            lambda i, c=c: q_in.at[c, i],
            lambda t, c=c: q_r.at[c, t],
            lambda t, c=c: q_l.at[c, t],
            lambda i, c=c: q_recv.at[c, i],
        )
        for c in range(chunks)
    ]
    kv_gather.start(0)
    pass_on(me, kv_ref)
    for gather in q_gathers:
        gather.start(0)
    kv_in[me] = kv_ref[...]

    key_pos = lax.broadcasted_iota(jnp.int32, (2 * rows, rows), 0)
    query_pos = lax.broadcasted_iota(jnp.int32, (2 * rows, rows), 1)
    low = jnp.where(ctx == 0, rows, 0)
    visible = (key_pos >= low) & (key_pos - rows <= query_pos)
    bias[...] = jnp.where(visible, F32(0.0), F32(-1e30))
    loads[0].wait()

    @pl.loop(0, heads)
    def _(h):
        at = pl.multiple_of(h * NOPE, NOPE)
        wkt[pl.ds(at, NOPE), :] = wk[:, pl.ds(at, NOPE)].T

    def kv_step(t):
        kv_gather.arrive(t, lambda owner: pass_on(owner, kv_in.at[owner]))

    def q_step(c, t):
        q_gathers[c].arrive(t)

    kv_step(0)
    loads[1].wait()

    @pl.loop(0, heads)
    def _(h):
        at = pl.multiple_of(h * VDIM, VDIM)
        wvt[pl.ds(at, VDIM), :] = wv[:, pl.ds(at, VDIM)].T

    def add_queries(c, block, owner, first=False):
        at = pl.multiple_of(owner * q_cols, q_cols)
        span = pl.ds(c * part_rows, part_rows)
        tile = 2 * WIDTH

        @pl.loop(0, wq.shape[1] // tile)
        def _(j):
            cols = pl.ds(pl.multiple_of(j * tile, tile), tile)
            part = nn(block[...], wq[pl.ds(at, q_cols), cols])
            if first:
                q_acc[span, cols] = part
            else:
                q_acc[span, cols] += part

    def add_arrived(c, t):
        q_gathers[c].each(t, lambda owner: add_queries(c, q_in.at[c, owner], owner))

    def assemble(parts, row):
        width = n_head * kv_cols
        total = None
        for i in range(n_head):
            dst = lax.broadcasted_iota(jnp.int32, (width, kv_cols), 0)
            src = lax.broadcasted_iota(jnp.int32, (width, kv_cols), 1) + i * kv_cols
            place = jnp.where(src == dst, F32(1.0), F32(0.0)).astype(BF16)
            term = nn(place, parts[i])
            total = term if total is None else total + term
        total = total.astype(BF16)
        span = slice(row, row + rows)
        lat_t[:, span] = total
        lat[span, :KVL] = total[:KVL].T
        lat[span, KVL:] = total[KVL:].T

    def expand(row):
        tile = 2 * NOPE
        span = slice(row, row + rows)

        @pl.loop(0, heads // 2)
        def _(j):
            cols = pl.ds(pl.multiple_of(j * tile, tile), tile)
            main = lat[span, :KVL]
            main_t = lat_t[:KVL, span]
            keys[span, cols] = nn(main, wk[:, cols]).astype(BF16)
            values[span, cols] = nn(main, wv[:, cols]).astype(BF16)
            keys_t[cols, span] = nn(wkt[cols, :], main_t).astype(BF16)
            values_t[cols, span] = nn(wvt[cols, :], main_t).astype(BF16)

    def finish_queries(c):
        @pl.loop(0, wq.shape[1] // NOPE)
        def _(j):
            at = pl.multiple_of(j * NOPE, NOPE)
            span = slice(c * part_rows, (c + 1) * part_rows)
            q_t[pl.ds(at, NOPE), span] = q_acc[span, pl.ds(at, NOPE)].astype(BF16).T

    if last > 0:
        q_step(0, 0)

    @pl.loop(0, heads)
    def _(h):
        at = pl.multiple_of(h * VDIM, VDIM)
        dot_t[pl.ds(at, VDIM), :] = do_ref[:, pl.ds(at, VDIM)].T

    loads[2].wait()
    for c in range(chunks):
        add_queries(c, q_ref.at[pl.ds(c * part_rows, part_rows), :], me, True)
    for t in range(1, last):
        kv_step(t)
        add_arrived(0, t - 1)
        if t < last - 1:
            q_step(0, t)
    assemble([kv_in[i] for i in range(n_head)], rows)
    expand(rows)
    for i in range(n_head):
        copy_of(kv_ref, kv_prev.at[i], p_send.at[i], p_recv.at[i], after).wait_recv()
    assemble([kv_prev[i] for i in range(n_head)], 0)
    expand(0)
    if last > 1:
        q_step(0, last - 1)
    if last > 0:
        add_arrived(0, last - 1)
    finish_queries(0)
    krope[...] = jnp.zeros_like(krope)

    def attend(c, h):
        seen = rows + (c + 1) * part_rows
        span = slice(c * part_rows, (c + 1) * part_rows)
        at = pl.multiple_of(h * NOPE, NOPE)
        q_at = pl.ds(pl.multiple_of(h * WIDTH, WIDTH), WIDTH)
        cols = pl.ds(at, NOPE)
        query_t = q_t[q_at, span]
        key = jnp.concatenate([keys[:seen, cols], lat[:seen, KVL:]], 1)
        scores = nn(key, query_t)
        scores = scores + bias[:seen, span]
        top = jnp.max(scores, 0, keepdims=True)
        expons = jnp.exp2((scores - top) * F32(SCALE * math.log2(math.e)))
        probs = expons * (F32(1.0) / jnp.sum(expons, 0, keepdims=True))
        probs_b = probs.astype(BF16)
        result = nn(values_t[cols, :seen], probs_b).astype(BF16)
        out_ref[cols, span] = result
        grad_out = dot_t[cols, span]
        row_dot = jnp.sum(grad_out.astype(F32) * result.astype(F32), 0, keepdims=True)
        dprob = nn(values[:seen, cols], grad_out)
        dscore = (probs * (dprob - row_dot) * F32(SCALE)).astype(BF16)
        key_t = jnp.concatenate([keys_t[cols, :seen], lat_t[KVL:, :seen]], 0)
        gq_t[q_at, span] = nn(key_t, dscore).astype(BF16)
        g_key = nt(dscore, query_t[:NOPE])
        g_rope = nt(query_t[NOPE:], dscore)
        g_value = nt(probs_b, grad_out)
        if c > 0:
            before_rows = rows + c * part_rows
            g_key = jnp.concatenate([g_key[:before_rows] + gk_sum[:, cols], g_key[before_rows:]], 0)
            g_value = jnp.concatenate([g_value[:before_rows] + gv_sum[:, cols], g_value[before_rows:]], 0)
            g_rope = jnp.concatenate([g_rope[:, :before_rows] + kr_sum[h], g_rope[:, before_rows:]], 1)
        if c + 1 < chunks:
            gk_sum[:, cols] = g_key
            gv_sum[:, cols] = g_value
            kr_sum[h] = g_rope
        else:
            gk[:, cols] = g_key.astype(BF16)
            gv[:, cols] = g_value.astype(BF16)
            krope[...] += g_rope.astype(BF16).astype(F32)

    def attention(c, hooks):
        groups = max(1, len(hooks) + 1)
        edges = [heads * g // groups for g in range(groups + 1)]
        for g in range(groups):
            @pl.loop(edges[g] // UNROLL, edges[g + 1] // UNROLL)
            def _(h):
                for u in range(UNROLL):
                    attend(c, h * UNROLL + u)

            if g < len(hooks):
                hooks[g]()

    class Reduce:
        def __init__(self, part, out, in_right, in_left, send, recv_right, recv_left, stages):
            self.part, self.out, self.send = part, out, send
            self.ways = (
                (in_right, recv_right, right, stages[0], has_left),
                (in_left, recv_left, left, stages[1], has_right),
            )

        def step(self, tick):
            for way, (slots, recv, device, stage, joined) in enumerate(self.ways):
                lag = me if way == 0 else last - me
                owner = last - (tick - lag) if way == 0 else tick - lag

                @pl.when(tick >= lag)
                def _():
                    stage[...] = self.part(owner)

                    @pl.when(joined)
                    def _():
                        copy_of(slots(owner), slots(owner), self.send(owner), recv(owner), device).wait_recv()
                        stage[...] += slots(owner)[...].astype(F32)

                    self.out(owner)[...] = stage[...].astype(BF16)
                    copy_of(self.out(owner), slots(owner), self.send(owner), recv(owner), device).start()

        def total(self, stage):
            stage[...] = self.part(me)
            for slots, recv, device, _, joined in self.ways:
                @pl.when(joined)
                def _():
                    copy_of(slots(me), slots(me), self.send(me), recv(me), device).wait_recv()
                    stage[...] += slots(me)[...].astype(F32)

        def finish(self):
            for i in range(n_head):
                @pl.when(me != i)
                def _():
                    slot = self.out(i)
                    copy_of(slot, slot, self.send(i), self.send(i), right).wait_send()

    def query_part(c):
        def part(owner):
            at = pl.multiple_of(owner * q_cols, q_cols)
            return nn(wq[pl.ds(at, q_cols), :], gq_t[:, c * part_rows:(c + 1) * part_rows])

        return part

    def kv_part(owner):
        return gkv_own[pl.ds(pl.multiple_of(owner * kv_cols, 8), kv_cols), :]

    q_reduces = [
        Reduce(
            query_part(c),
            lambda i, c=c: rq_out.at[c, i],
            lambda i, c=c: rq_right.at[c, i],
            lambda i, c=c: rq_left.at[c, i],
            lambda i, c=c: rq_send.at[c, i],
            lambda i, c=c: rq_rr.at[c, i],
            lambda i, c=c: rq_rl.at[c, i],
            (stage_right, stage_left),
        )
        for c in range(chunks)
    ]
    kv_stage = (gkv_ref, gkv_ref)
    kv_reduce = Reduce(
        kv_part,
        lambda i: rkv_out.at[i],
        lambda i: rkv_right.at[i],
        lambda i: rkv_left.at[i],
        lambda i: rkv_send.at[i],
        lambda i: rkv_rr.at[i],
        lambda i: rkv_rl.at[i],
        kv_stage,
    )

    for c in range(chunks):
        hooks = []
        if c + 1 < chunks:
            hooks += [functools.partial(q_step, c + 1, t) for t in range(last)]
        if c > 0:
            hooks += [functools.partial(q_reduces[c - 1].step, t) for t in range(last)]
        attention(c, hooks)
        if c + 1 < chunks:
            for t in range(last):
                add_arrived(c + 1, t)
            finish_queries(c + 1)

    def project(row):
        return nt(wk[...], gk[row:row + rows, :]) + nt(wv[...], gv[row:row + rows, :])

    final = q_reduces[chunks - 1]
    if last > 0:
        final.step(0)
    back_out[:KVL, :] = project(0).astype(BF16)
    back_out[KVL:, :] = krope[:, :rows].astype(BF16)
    back = copy_of(back_out, back_in, b_send, b_recv, before)
    back.start()
    gkv_own[:KVL, :] = project(rows)
    gkv_own[KVL:, :] = krope[:, rows:]
    if last > 1:
        final.step(1)
    back.wait_recv()
    gkv_own[...] += back_in[...].astype(F32)
    for t in range(last):
        kv_reduce.step(t)
        if t + 2 < last:
            final.step(t + 2)

    for c in range(chunks):
        q_reduces[c].total(stage_right)
        gq_ref[:, c * part_rows:(c + 1) * part_rows] = stage_right[...]
    kv_reduce.total(gkv_ref)

    kv_gather.finish()
    kv_reduce.finish()
    for c in range(chunks):
        q_gathers[c].finish()
        q_reduces[c].finish()
    for i in range(n_head):
        copy_of(kv_ref, kv_prev.at[i], p_send.at[i], p_recv.at[i], after).wait_send()
    back.wait_send()


CHUNKS = 1
UNROLL = 2


def on_device(n_ctx, n_head, q_latent, kv_latent, w_query, w_key, w_value, d_out):
    rows, q_cols = q_latent.shape
    kv_cols = kv_latent.shape[1]
    ql, qw = w_query.shape
    kw = w_key.shape[1]
    kvw = n_head * kv_cols
    heads = kw // NOPE
    part_rows = rows // CHUNKS
    held = 2 * rows - part_rows if CHUNKS > 1 else 8
    vmem = pl.BlockSpec(memory_space=pltpu.VMEM)
    hbm = pl.BlockSpec(memory_space=pl.ANY)
    dma = pltpu.SemaphoreType.DMA
    some = (n_head,)
    each = (CHUNKS, n_head)
    out_t, gq_t, gkv_t = pl.pallas_call(
        functools.partial(kernel, n_ctx, n_head, CHUNKS),
        out_shape=(
            jax.ShapeDtypeStruct((kw, rows), BF16),
            jax.ShapeDtypeStruct((q_cols, rows), F32),
            jax.ShapeDtypeStruct((kv_cols, rows), F32),
        ),
        in_specs=[vmem, vmem, vmem, hbm, hbm, hbm],
        out_specs=(vmem, vmem, vmem),
        scratch_shapes=[
            pltpu.VMEM((ql, qw), BF16),
            pltpu.VMEM((KVL, kw), BF16),
            pltpu.VMEM((KVL, kw), BF16),
            pltpu.VMEM((kw, KVL), BF16),
            pltpu.VMEM((kw, KVL), BF16),
            pltpu.VMEM((kw, rows), BF16),
            pltpu.VMEM((CHUNKS, n_head, part_rows, q_cols), BF16),
            pltpu.VMEM((n_head, kv_cols, rows), BF16),
            pltpu.VMEM((n_head, kv_cols, rows), BF16),
            pltpu.VMEM((2 * rows, kvw), BF16),
            pltpu.VMEM((kvw, 2 * rows), BF16),
            pltpu.VMEM((rows, qw), F32),
            pltpu.VMEM((qw, rows), BF16),
            pltpu.VMEM((2 * rows, kw), BF16),
            pltpu.VMEM((kw, 2 * rows), BF16),
            pltpu.VMEM((2 * rows, kw), BF16),
            pltpu.VMEM((kw, 2 * rows), BF16),
            pltpu.VMEM((qw, rows), BF16),
            pltpu.VMEM((2 * rows, kw), BF16),
            pltpu.VMEM((2 * rows, kw), BF16),
            pltpu.VMEM((held, kw), F32),
            pltpu.VMEM((held, kw), F32),
            pltpu.VMEM((heads, ROPE, held), F32),
            pltpu.VMEM((ROPE, 2 * rows), F32),
            pltpu.VMEM((kvw, rows), BF16),
            pltpu.VMEM((kvw, rows), BF16),
            pltpu.VMEM((CHUNKS, n_head, q_cols, part_rows), BF16),
            pltpu.VMEM((CHUNKS, n_head, q_cols, part_rows), BF16),
            pltpu.VMEM((CHUNKS, n_head, q_cols, part_rows), BF16),
            pltpu.VMEM((n_head, kv_cols, rows), BF16),
            pltpu.VMEM((n_head, kv_cols, rows), BF16),
            pltpu.VMEM((n_head, kv_cols, rows), BF16),
            pltpu.VMEM((kvw, rows), F32),
            pltpu.VMEM((q_cols, part_rows), F32),
            pltpu.VMEM((q_cols, part_rows), F32),
            pltpu.VMEM((2 * rows, rows), F32),
            dma((3,)),
            dma(some), dma(some), dma(some),
            dma(each), dma(each), dma(each),
            dma(some), dma(some),
            dma, dma,
            dma(each), dma(each), dma(each),
            dma(some), dma(some), dma(some),
        ],
        compiler_params=pltpu.CompilerParams(
            collective_id=0, has_side_effects=True, vmem_limit_bytes=62 * 1024 * 1024,
        ),
        name="latent_attention",
    )(q_latent, kv_latent.T, d_out, w_query, w_key, w_value)
    return out_t.T, gq_t.T, gkv_t.T


def solution(mesh):
    return jax.shard_map(
        functools.partial(on_device, mesh.shape["ctx"], mesh.shape["head"]),
        mesh=mesh,
        in_specs=(
            P("ctx", "head"),
            P("ctx", "head"),
            P(None, "head"),
            P(None, "head"),
            P(None, "head"),
            P("ctx", "head"),
        ),
        out_specs=(P("ctx", "head"), P("ctx", "head"), P("ctx", "head")),
        check_vma=False,
    )
```

profile of v0, /device:TPU:0, one launch (start us, length us, event | category | flops | bytes accessed | tf_op | source)
XLA Modules:
  0.0 80.1 jit_solution(3705723458183220586)
XLA Ops:
  0.6 75.5 %latent_attention.1 = (bf16[2048,256]{1,0:T(8,128)(2,1)}, f32[384,256]{1,0:T(8,128)}, f32[144,256]{1,0:T(8,128)}) custom-call(bf16[256,384]{1,0:T(8,128)(2,1)} %q_ref.1, bf16[144,256]{1,0:T(8,128)(2,1)} %bitcast.7, bf16[256,2048]{1,0:T(8,128)(2,1)} %do_ref.1, bf16[1536,3072]{1,0:T(8,128)(2,1)} %wq_hbm.1, bf16[512,2048]{1,0:T(8,128)(2,1)} %wk_hbm.1, ...), custom_call_target="tpu_custom_call" | custom-call | tf_op jit(solution)/shard_map/latent_attention/pallas_call | solution.py:446
  76.2 0.0 copy-start
  76.2 0.0 copy-start.1
  76.2 2.3 %copy.9 = bf16[256,2048]{1,0:T(8,128)(2,1)} copy(bf16[256,2048]{0,1:T(8,128)(2,1)} %bitcast.4) | data formatting | bytes 2097152
  78.5 0.0 copy-done
  78.5 0.9 %copy.10 = f32[256,384]{1,0:T(8,128)} copy(f32[256,384]{0,1:T(8,128)S(1)} %bitcast.5) | data formatting | bytes 786432
  79.4 0.0 copy-done.1
  79.5 0.7 copy.12
Async XLA Ops:
  76.2 2.3 %copy-start = (f32[384,256]{1,0:T(8,128)S(1)}, f32[384,256]{1,0:T(8,128)}, u32[]{:S(2)}) copy-start(f32[384,256]{1,0:T(8,128)} %get-tuple-element.7) | copy-start | bytes 1179652
  76.2 3.3 %copy-start.1 = (f32[144,256]{1,0:T(8,128)S(1)}, f32[144,256]{1,0:T(8,128)}, u32[]{:S(2)}) copy-start(f32[144,256]{1,0:T(8,128)} %get-tuple-element.8) | copy-start | bytes 442372
where the time goes:
time: 80.5 us; the launch traced here: 80.1 us
  Pallas kernels  75.5 us (94%)
  local copies, waits for them, and re-layouts  3.91 us (5%)
    pallas_call x1, Pallas kernels, on_device(): pl.pallas_call(functools.partial(kernel, n_ctx, n_head, CHUNKS), out_shap...  75.5 us
    unnamed x7, local copies, waits for them, and re-layouts  3.91 us

commit v1 on v0

--- a/solution.py
+++ b/solution.py
@@ -28,11 +28,11 @@
 
 
 def kernel(
-    n_ctx, n_head, chunks,
+    n_ctx, n_head,
     q_ref, kv_ref, do_ref, wq_hbm, wk_hbm, wv_hbm,
     out_ref, gq_ref, gkv_ref,
-    wq, wk, wv, wkt, wvt, dot_t, q_in, kv_in, kv_prev, lat, lat_t, q_acc, q_t,
-    keys, keys_t, values, values_t, gq_t, gk, gv, gk_sum, gv_sum, kr_sum, krope, back_out, back_in,
+    wq, wk, wv, wkt, wvt, dot_t, q_in, kv_in, kv_prev, lat_t, q_acc, q_b,
+    keys_t, values_t, s_buf, dp_buf, p_buf, pb_all, ds_all, gq_t, gk_t, gv_t, krope, back_out, back_in,
     rq_out, rq_right, rq_left, rkv_out, rkv_right, rkv_left, gkv_own, stage_right, stage_left,
     bias, w_sem, kv_r, kv_l, kv_recv, q_r, q_l, q_recv, p_send, p_recv,
     b_send, b_recv, rq_send, rq_rr, rq_rl, rkv_send, rkv_rr, rkv_rl,
@@ -41,7 +41,7 @@
     me = lax.axis_index("head")
     last = n_head - 1
     rows, q_cols = q_ref.shape
-    part_rows = rows // chunks
+    part_rows = rows // CHUNKS
     kv_cols = kv_ref.shape[0]
     heads = wk.shape[1] // NOPE
     after = {"ctx": lax.rem(ctx + 1, n_ctx)}
@@ -135,25 +135,29 @@
             lambda t, c=c: q_l.at[c, t],
             lambda i, c=c: q_recv.at[c, i],
         )
-        for c in range(chunks)
+        for c in range(CHUNKS)
     ]
     kv_gather.start(0)
+    q_gathers[0].start(0)
     pass_on(me, kv_ref)
-    for gather in q_gathers:
-        gather.start(0)
     kv_in[me] = kv_ref[...]
 
-    key_pos = lax.broadcasted_iota(jnp.int32, (2 * rows, rows), 0)
-    query_pos = lax.broadcasted_iota(jnp.int32, (2 * rows, rows), 1)
-    low = jnp.where(ctx == 0, rows, 0)
-    visible = (key_pos >= low) & (key_pos - rows <= query_pos)
-    bias[...] = jnp.where(visible, F32(0.0), F32(-1e30))
-    loads[0].wait()
-
-    @pl.loop(0, heads)
-    def _(h):
-        at = pl.multiple_of(h * NOPE, NOPE)
-        wkt[pl.ds(at, NOPE), :] = wk[:, pl.ds(at, NOPE)].T
+    key_pos = lax.broadcasted_iota(jnp.int32, (part_rows, part_rows), 1)
+    query_pos = lax.broadcasted_iota(jnp.int32, (part_rows, part_rows), 0)
+    bias[...] = jnp.where(key_pos <= query_pos, F32(0.0), F32(-1e30))
+    prev_mask = jnp.where(ctx == 0, F32(-1e30), F32(0.0))
+    for c in range(CHUNKS - 1):
+        seen = rows + (c + 1) * part_rows
+        unseen = jnp.zeros((heads, part_rows, 2 * rows - seen), BF16)
+        pb_all[:, c * part_rows:(c + 1) * part_rows, seen:] = unseen
+        ds_all[:, c * part_rows:(c + 1) * part_rows, seen:] = unseen
+
+    def turn(src, dst):
+        @pl.loop(0, heads // 2)
+        def _(j):
+            for u in range(2):
+                at = pl.multiple_of((2 * j + u) * NOPE, NOPE)
+                dst[pl.ds(at, NOPE), :] = src[:, pl.ds(at, NOPE)].T
 
     def kv_step(t):
         kv_gather.arrive(t, lambda owner: pass_on(owner, kv_in.at[owner]))
@@ -161,32 +165,34 @@
     def q_step(c, t):
         q_gathers[c].arrive(t)
 
-    kv_step(0)
-    loads[1].wait()
-
-    @pl.loop(0, heads)
-    def _(h):
-        at = pl.multiple_of(h * VDIM, VDIM)
-        wvt[pl.ds(at, VDIM), :] = wv[:, pl.ds(at, VDIM)].T
-
     def add_queries(c, block, owner, first=False):
         at = pl.multiple_of(owner * q_cols, q_cols)
-        span = pl.ds(c * part_rows, part_rows)
-        tile = 2 * WIDTH
+        tile = 4 * WIDTH
 
         @pl.loop(0, wq.shape[1] // tile)
         def _(j):
             cols = pl.ds(pl.multiple_of(j * tile, tile), tile)
             part = nn(block[...], wq[pl.ds(at, q_cols), cols])
             if first:
-                q_acc[span, cols] = part
+                q_acc[:, cols] = part
             else:
-                q_acc[span, cols] += part
+                q_acc[:, cols] += part
+
+    def own_queries(c):
+        add_queries(c, q_ref.at[pl.ds(c * part_rows, part_rows), :], me, True)
 
     def add_arrived(c, t):
         q_gathers[c].each(t, lambda owner: add_queries(c, q_in.at[c, owner], owner))
 
+    def finish_queries(c):
+        q_b[c * part_rows:(c + 1) * part_rows, :] = q_acc[...].astype(BF16)
+
     def assemble(parts, row):
+        span = slice(row, row + rows)
+        if kv_cols % 16 == 0:
+            for i in range(n_head):
+                lat_t[i * kv_cols:(i + 1) * kv_cols, span] = parts[i]
+            return
         width = n_head * kv_cols
         total = None
         for i in range(n_head):
@@ -195,112 +201,110 @@
             place = jnp.where(src == dst, F32(1.0), F32(0.0)).astype(BF16)
             term = nn(place, parts[i])
             total = term if total is None else total + term
-        total = total.astype(BF16)
+        lat_t[:, span] = total.astype(BF16)
+
+    def expand(row):
+        tile = 4 * NOPE
         span = slice(row, row + rows)
-        lat_t[:, span] = total
-        lat[span, :KVL] = total[:KVL].T
-        lat[span, KVL:] = total[KVL:].T
-
-    def expand(row):
-        tile = 2 * NOPE
-        span = slice(row, row + rows)
-
-        @pl.loop(0, heads // 2)
+
+        @pl.loop(0, heads // 4)
         def _(j):
             cols = pl.ds(pl.multiple_of(j * tile, tile), tile)
-            main = lat[span, :KVL]
             main_t = lat_t[:KVL, span]
-            keys[span, cols] = nn(main, wk[:, cols]).astype(BF16)
-            values[span, cols] = nn(main, wv[:, cols]).astype(BF16)
             keys_t[cols, span] = nn(wkt[cols, :], main_t).astype(BF16)
             values_t[cols, span] = nn(wvt[cols, :], main_t).astype(BF16)
 
-    def finish_queries(c):
-        @pl.loop(0, wq.shape[1] // NOPE)
-        def _(j):
-            at = pl.multiple_of(j * NOPE, NOPE)
-            span = slice(c * part_rows, (c + 1) * part_rows)
-            q_t[pl.ds(at, NOPE), span] = q_acc[span, pl.ds(at, NOPE)].astype(BF16).T
-
-    if last > 0:
-        q_step(0, 0)
-
-    @pl.loop(0, heads)
-    def _(h):
-        at = pl.multiple_of(h * VDIM, VDIM)
-        dot_t[pl.ds(at, VDIM), :] = do_ref[:, pl.ds(at, VDIM)].T
-
-    loads[2].wait()
-    for c in range(chunks):
-        add_queries(c, q_ref.at[pl.ds(c * part_rows, part_rows), :], me, True)
-    for t in range(1, last):
-        kv_step(t)
-        add_arrived(0, t - 1)
-        if t < last - 1:
-            q_step(0, t)
-    assemble([kv_in[i] for i in range(n_head)], rows)
-    expand(rows)
-    for i in range(n_head):
-        copy_of(kv_ref, kv_prev.at[i], p_send.at[i], p_recv.at[i], after).wait_recv()
-    assemble([kv_prev[i] for i in range(n_head)], 0)
-    expand(0)
-    if last > 1:
-        q_step(0, last - 1)
-    if last > 0:
-        add_arrived(0, last - 1)
-    finish_queries(0)
-    krope[...] = jnp.zeros_like(krope)
-
-    def attend(c, h):
-        seen = rows + (c + 1) * part_rows
-        span = slice(c * part_rows, (c + 1) * part_rows)
-        at = pl.multiple_of(h * NOPE, NOPE)
-        q_at = pl.ds(pl.multiple_of(h * WIDTH, WIDTH), WIDTH)
-        cols = pl.ds(at, NOPE)
-        query_t = q_t[q_at, span]
-        key = jnp.concatenate([keys[:seen, cols], lat[:seen, KVL:]], 1)
-        scores = nn(key, query_t)
-        scores = scores + bias[:seen, span]
-        top = jnp.max(scores, 0, keepdims=True)
-        expons = jnp.exp2((scores - top) * F32(SCALE * math.log2(math.e)))
-        probs = expons * (F32(1.0) / jnp.sum(expons, 0, keepdims=True))
-        probs_b = probs.astype(BF16)
-        result = nn(values_t[cols, :seen], probs_b).astype(BF16)
-        out_ref[cols, span] = result
-        grad_out = dot_t[cols, span]
-        row_dot = jnp.sum(grad_out.astype(F32) * result.astype(F32), 0, keepdims=True)
-        dprob = nn(values[:seen, cols], grad_out)
-        dscore = (probs * (dprob - row_dot) * F32(SCALE)).astype(BF16)
-        key_t = jnp.concatenate([keys_t[cols, :seen], lat_t[KVL:, :seen]], 0)
-        gq_t[q_at, span] = nn(key_t, dscore).astype(BF16)
-        g_key = nt(dscore, query_t[:NOPE])
-        g_rope = nt(query_t[NOPE:], dscore)
-        g_value = nt(probs_b, grad_out)
-        if c > 0:
-            before_rows = rows + c * part_rows
-            g_key = jnp.concatenate([g_key[:before_rows] + gk_sum[:, cols], g_key[before_rows:]], 0)
-            g_value = jnp.concatenate([g_value[:before_rows] + gv_sum[:, cols], g_value[before_rows:]], 0)
-            g_rope = jnp.concatenate([g_rope[:, :before_rows] + kr_sum[h], g_rope[:, before_rows:]], 1)
-        if c + 1 < chunks:
-            gk_sum[:, cols] = g_key
-            gv_sum[:, cols] = g_value
-            kr_sum[h] = g_rope
-        else:
-            gk[:, cols] = g_key.astype(BF16)
-            gv[:, cols] = g_value.astype(BF16)
-            krope[...] += g_rope.astype(BF16).astype(F32)
+    def window(h, odd):
+        first = (h - 1 if odd else h) * WIDTH + (NOPE if odd else 0)
+        return pl.ds(pl.multiple_of(first, NOPE), WIDTH + ROPE)
+
+    def columns(h):
+        return pl.ds(pl.multiple_of(h * NOPE, NOPE), NOPE)
+
+    def seen_by(c):
+        return rows + (c + 1) * part_rows
+
+    def span_of(c):
+        return slice(c * part_rows, (c + 1) * part_rows)
+
+    def pieces(c):
+        return [
+            (slice(r, r + PIECE), slice(c * part_rows + r, c * part_rows + r + PIECE))
+            for r in range(0, part_rows, PIECE)
+        ]
+
+    def score_stage(c, h, odd):
+        seen = seen_by(c)
+        query = q_b[span_of(c), window(h, odd)]
+        key = [keys_t[columns(h), :seen], lat_t[KVL:, :seen]]
+        pad = [jnp.zeros((ROPE, seen), BF16)]
+        s_buf[:, :seen] = nn(query, jnp.concatenate(pad + key if odd else key + pad, 0))
+
+    def softmax_stage(c, h):
+        seen = seen_by(c)
+        dp_buf[:, :seen] = nn(do_ref[span_of(c), columns(h)], values_t[columns(h), :seen])
+        for sub, row in pieces(c):
+            scores = [s_buf[sub, :rows] + prev_mask]
+            if c > 0:
+                scores.append(s_buf[sub, rows:seen - part_rows])
+            scores.append(s_buf[sub, seen - part_rows:seen] + bias[sub, :])
+            scores = jnp.concatenate(scores, 1)
+            top = jnp.max(scores, 1, keepdims=True)
+            expons = jnp.exp2((scores - top) * F32(SCALE * math.log2(math.e)))
+            probs = expons * (F32(1.0) / jnp.sum(expons, 1, keepdims=True))
+            p_buf[sub, :seen] = probs
+            pb_all[h, row, :seen] = probs.astype(BF16)
+
+    def output_stage(c, h):
+        seen = seen_by(c)
+        span = span_of(c)
+        cols = columns(h)
+        result = nt(pb_all[h, span, :seen], values_t[cols, :seen]).astype(BF16)
+        out_ref[span, cols] = result
+        row_dot = jnp.sum(do_ref[span, cols].astype(F32) * result.astype(F32), 1, keepdims=True)
+        for sub, row in pieces(c):
+            dscore = p_buf[sub, :seen] * (dp_buf[sub, :seen] - row_dot[sub]) * F32(SCALE)
+            ds_all[h, row, :seen] = dscore.astype(BF16)
+
+    def gradient_stage(c, h, odd, valid):
+        seen = seen_by(c)
+        span = span_of(c)
+        cols = columns(h)
+        key = jnp.concatenate([keys_t[cols, :seen], lat_t[KVL:, :seen]], 0)
+        q_at = pl.ds(pl.multiple_of(h * WIDTH, ROPE), WIDTH)
+        gq_t[q_at, span] = nt(key, ds_all[h, span, :seen]).astype(BF16)
+        if c + 1 < CHUNKS:
+            return
+        query_t = q_b[:, window(h, odd)].T
+        query_t = query_t[ROPE:] if odd else query_t[:WIDTH]
+        g_key = nn(query_t, ds_all[h])
+        gk_t[cols, :] = g_key[:NOPE].astype(BF16)
+        g_rope = g_key[NOPE:].astype(BF16).astype(F32)
+        krope[...] += g_rope if valid is None else jnp.where(valid, g_rope, F32(0.0))
+        gv_t[cols, :] = nn(dot_t[cols, :], pb_all[h]).astype(BF16)
 
     def attention(c, hooks):
-        groups = max(1, len(hooks) + 1)
-        edges = [heads * g // groups for g in range(groups + 1)]
-        for g in range(groups):
-            @pl.loop(edges[g] // UNROLL, edges[g + 1] // UNROLL)
-            def _(h):
-                for u in range(UNROLL):
-                    attend(c, h * UNROLL + u)
-
-            if g < len(hooks):
-                hooks[g]()
+        trips = heads // 2
+        count = len(hooks) + 1
+
+        @pl.loop(0, trips)
+        def _(t):
+            for i, hook in enumerate(hooks):
+                pl.when(t == trips * (i + 1) // count)(hook)
+            for u in range(2):
+                odd = u == 1
+                step = 2 * t + u
+                gradient_stage(c, jnp.maximum(step - 3, 0 if odd else 1), not odd, step >= 3)
+                output_stage(c, jnp.maximum(step - 2, 0))
+                softmax_stage(c, jnp.maximum(step - 1, 0))
+                score_stage(c, step, odd)
+
+        gradient_stage(c, heads - 3, True, None)
+        output_stage(c, heads - 2)
+        softmax_stage(c, heads - 1)
+        gradient_stage(c, heads - 2, False, None)
+        output_stage(c, heads - 1)
+        gradient_stage(c, heads - 1, True, None)
 
     class Reduce:
         def __init__(self, part, out, in_right, in_left, send, recv_right, recv_left, stages):
@@ -363,7 +367,7 @@
             lambda i, c=c: rq_rl.at[c, i],
             (stage_right, stage_left),
         )
-        for c in range(chunks)
+        for c in range(CHUNKS)
     ]
     kv_stage = (gkv_ref, gkv_ref)
     kv_reduce = Reduce(
@@ -377,47 +381,79 @@
         kv_stage,
     )
 
-    for c in range(chunks):
-        hooks = []
-        if c + 1 < chunks:
-            hooks += [functools.partial(q_step, c + 1, t) for t in range(last)]
-        if c > 0:
-            hooks += [functools.partial(q_reduces[c - 1].step, t) for t in range(last)]
-        attention(c, hooks)
-        if c + 1 < chunks:
-            for t in range(last):
-                add_arrived(c + 1, t)
-            finish_queries(c + 1)
+    loads[0].wait()
+    turn(wk, wkt)
+    if last > 0:
+        kv_step(0)
+    loads[1].wait()
+    turn(wv, wvt)
+    if last > 0:
+        q_step(0, 0)
+    turn(do_ref, dot_t)
+    for t in range(1, last - 1):
+        kv_step(t)
+    loads[2].wait()
+    own_queries(0)
+    for t in range(1, last):
+        add_arrived(0, t - 1)
+        q_step(0, t)
+        if t == max(1, last - 2):
+            q_gathers[1].start(0)
+    if last > 1:
+        kv_step(last - 1)
+    assemble([kv_in[i] for i in range(n_head)], rows)
+    expand(rows)
+    for i in range(n_head):
+        copy_of(kv_ref, kv_prev.at[i], p_send.at[i], p_recv.at[i], after).wait_recv()
+    assemble([kv_prev[i] for i in range(n_head)], 0)
+    expand(0)
+    if last > 0:
+        add_arrived(0, last - 1)
+    finish_queries(0)
+    krope[...] = jnp.zeros_like(krope)
+    if last > 0:
+        q_step(1, 0)
+    attention(0, [functools.partial(q_step, 1, t) for t in range(1, last)])
+    if last > 0:
+        q_reduces[0].step(0)
+    own_queries(1)
+    for t in range(last):
+        add_arrived(1, t)
+    finish_queries(1)
+    attention(1, [functools.partial(q_reduces[0].step, t) for t in range(1, last)])
 
     def project(row):
-        return nt(wk[...], gk[row:row + rows, :]) + nt(wv[...], gv[row:row + rows, :])
-
-    final = q_reduces[chunks - 1]
+        span = slice(row, row + rows)
+        return nn(wk[...], gk_t[:, span]) + nn(wv[...], gv_t[:, span])
+
+    final = q_reduces[1]
     if last > 0:
         final.step(0)
     back_out[:KVL, :] = project(0).astype(BF16)
     back_out[KVL:, :] = krope[:, :rows].astype(BF16)
     back = copy_of(back_out, back_in, b_send, b_recv, before)
     back.start()
+    if last > 1:
+        final.step(1)
     gkv_own[:KVL, :] = project(rows)
     gkv_own[KVL:, :] = krope[:, rows:]
-    if last > 1:
-        final.step(1)
+    if last > 2:
+        final.step(2)
     back.wait_recv()
     gkv_own[...] += back_in[...].astype(F32)
     for t in range(last):
         kv_reduce.step(t)
-        if t + 2 < last:
-            final.step(t + 2)
-
-    for c in range(chunks):
+        if t + 3 < last:
+            final.step(t + 3)
+
+    for c in range(CHUNKS):
         q_reduces[c].total(stage_right)
         gq_ref[:, c * part_rows:(c + 1) * part_rows] = stage_right[...]
     kv_reduce.total(gkv_ref)
 
     kv_gather.finish()
     kv_reduce.finish()
-    for c in range(chunks):
+    for c in range(CHUNKS):
         q_gathers[c].finish()
         q_reduces[c].finish()
     for i in range(n_head):
@@ -425,8 +461,8 @@
     back.wait_send()
 
 
-CHUNKS = 1
-UNROLL = 2
+CHUNKS = 2
+PIECE = 32
 
 
 def on_device(n_ctx, n_head, q_latent, kv_latent, w_query, w_key, w_value, d_out):
@@ -437,16 +473,15 @@
     kvw = n_head * kv_cols
     heads = kw // NOPE
     part_rows = rows // CHUNKS
-    held = 2 * rows - part_rows if CHUNKS > 1 else 8
     vmem = pl.BlockSpec(memory_space=pltpu.VMEM)
     hbm = pl.BlockSpec(memory_space=pl.ANY)
     dma = pltpu.SemaphoreType.DMA
     some = (n_head,)
     each = (CHUNKS, n_head)
-    out_t, gq_t, gkv_t = pl.pallas_call(
-        functools.partial(kernel, n_ctx, n_head, CHUNKS),
+    out, gq_t, gkv_t = pl.pallas_call(
+        functools.partial(kernel, n_ctx, n_head),
         out_shape=(
-            jax.ShapeDtypeStruct((kw, rows), BF16),
+            jax.ShapeDtypeStruct((rows, kw), BF16),
             jax.ShapeDtypeStruct((q_cols, rows), F32),
             jax.ShapeDtypeStruct((kv_cols, rows), F32),
         ),
@@ -462,20 +497,19 @@
             pltpu.VMEM((CHUNKS, n_head, part_rows, q_cols), BF16),
             pltpu.VMEM((n_head, kv_cols, rows), BF16),
             pltpu.VMEM((n_head, kv_cols, rows), BF16),
-            pltpu.VMEM((2 * rows, kvw), BF16),
             pltpu.VMEM((kvw, 2 * rows), BF16),
-            pltpu.VMEM((rows, qw), F32),
+            pltpu.VMEM((part_rows, qw), F32),
+            pltpu.VMEM((rows, qw), BF16),
+            pltpu.VMEM((kw, 2 * rows), BF16),
+            pltpu.VMEM((kw, 2 * rows), BF16),
+            pltpu.VMEM((part_rows, 2 * rows), F32),
+            pltpu.VMEM((part_rows, 2 * rows), F32),
+            pltpu.VMEM((part_rows, 2 * rows), F32),
+            pltpu.VMEM((heads, rows, 2 * rows), BF16),
+            pltpu.VMEM((heads, rows, 2 * rows), BF16),
             pltpu.VMEM((qw, rows), BF16),
-            pltpu.VMEM((2 * rows, kw), BF16),
             pltpu.VMEM((kw, 2 * rows), BF16),
-            pltpu.VMEM((2 * rows, kw), BF16),
             pltpu.VMEM((kw, 2 * rows), BF16),
-            pltpu.VMEM((qw, rows), BF16),
-            pltpu.VMEM((2 * rows, kw), BF16),
-            pltpu.VMEM((2 * rows, kw), BF16),
-            pltpu.VMEM((held, kw), F32),
-            pltpu.VMEM((held, kw), F32),
-            pltpu.VMEM((heads, ROPE, held), F32),
             pltpu.VMEM((ROPE, 2 * rows), F32),
             pltpu.VMEM((kvw, rows), BF16),
             pltpu.VMEM((kvw, rows), BF16),
@@ -488,7 +522,7 @@
             pltpu.VMEM((kvw, rows), F32),
             pltpu.VMEM((q_cols, part_rows), F32),
             pltpu.VMEM((q_cols, part_rows), F32),
-            pltpu.VMEM((2 * rows, rows), F32),
+            pltpu.VMEM((part_rows, part_rows), F32),
             dma((3,)),
             dma(some), dma(some), dma(some),
             dma(each), dma(each), dma(each),
@@ -502,7 +536,7 @@
         ),
         name="latent_attention",
     )(q_latent, kv_latent.T, d_out, w_query, w_key, w_value)
-    return out_t.T, gq_t.T, gkv_t.T
+    return out, gq_t.T, gkv_t.T
 
 
 def solution(mesh):

time: 80.5 us -> 74 us (0.919)
  Pallas kernels: 75.5 us -> 68.2 us
  local copies, waits for them, and re-layouts: 3.91 us -> 4.91 us
    pallas_call x1, Pallas kernels: 75.5 us -> 68.2 us  [on_device(): pl.pallas_call(functools.partial(kernel, n_ctx, n_head), out_shape=(jax.S...]
    unnamed x7 -> x5, local copies, waits for them, and re-layouts: 3.91 us -> 4.91 us
where the time goes in v1:
time: 74 us; the launch traced here: 73.8 us
  Pallas kernels  68.2 us (92%)
  local copies, waits for them, and re-layouts  4.91 us (7%)
    pallas_call x1, Pallas kernels, on_device(): pl.pallas_call(functools.partial(kernel, n_ctx, n_head), out_shape=(jax.S...  68.2 us
    unnamed x5, local copies, waits for them, and re-layouts  4.91 us

profile of v1, /device:TPU:0, one launch (start us, length us, event | category | flops | bytes accessed | tf_op | source)
XLA Modules:
  0.0 73.8 jit_solution(12014757260777861004)
XLA Ops:
  0.6 68.2 %latent_attention.1 = (bf16[256,2048]{1,0:T(8,128)(2,1)}, f32[384,256]{1,0:T(8,128)}, f32[144,256]{1,0:T(8,128)}) custom-call(bf16[256,384]{1,0:T(8,128)(2,1)} %q_ref.1, bf16[144,256]{1,0:T(8,128)(2,1)} %bitcast.5, bf16[256,2048]{1,0:T(8,128)(2,1)} %do_ref.1, bf16[1536,3072]{1,0:T(8,128)(2,1)} %wq_hbm.1, bf16[512,2048]{1,0:T(8,128)(2,1)} %wk_hbm.1, ...), custom_call_target="tpu_custom_call" | custom-call | tf_op jit(solution)/shard_map/latent_attention/pallas_call | solution.py:481
  68.9 0.0 copy-start
  68.9 1.9 %copy.9 = f32[256,384]{1,0:T(8,128)} copy(f32[256,384]{0,1:T(8,128)} %bitcast.3) | data formatting | bytes 786432
  70.8 2.3 %copy.12 = bf16[256,2048]{1,0:T(8,128)(2,1)} copy(bf16[256,2048]{1,0:T(8,128)(2,1)} %get-tuple-element.15) | data formatting | bytes 2097152
  73.1 0.0 copy-done
  73.1 0.7 copy.13
Async XLA Ops:
  68.9 4.3 %copy-start = (f32[144,256]{1,0:T(8,128)S(1)}, f32[144,256]{1,0:T(8,128)}, u32[]{:S(2)}) copy-start(f32[144,256]{1,0:T(8,128)} %get-tuple-element.8) | copy-start | bytes 442372

commit v2 on v1

--- a/solution.py
+++ b/solution.py
@@ -29,11 +29,11 @@
 
 def kernel(
     n_ctx, n_head,
-    q_ref, kv_ref, do_ref, wq_hbm, wk_hbm, wv_hbm,
+    q_hbm, kv_hbm, do_hbm, wq_hbm, wk_hbm, wv_hbm,
     out_ref, gq_ref, gkv_ref,
-    wq, wk, wv, wkt, wvt, dot_t, q_in, kv_in, kv_prev, lat_t, q_acc, q_b,
+    q_ref, kv_ref, do_ref, wq, wk, wv, wkt, wvt, dot_t, q_in, kv_in, kv_prev, lat_t, q_acc, q_b,
     keys_t, values_t, s_buf, dp_buf, p_buf, pb_all, ds_all, gq_t, gk_t, gv_t, krope, back_out, back_in,
-    rq_out, rq_right, rq_left, rkv_out, rkv_right, rkv_left, gkv_own, stage_right, stage_left,
+    rq_out, rq_right, rq_left, rkv_out, rkv_right, rkv_left, gkv_own, stage_right, stage_left, stage_own,
     bias, w_sem, kv_r, kv_l, kv_recv, q_r, q_l, q_recv, p_send, p_recv,
     b_send, b_recv, rq_send, rq_rr, rq_rl, rkv_send, rkv_rr, rkv_rl,
 ):
@@ -53,7 +53,9 @@
 
     loads = [
         pltpu.make_async_copy(src, dst, w_sem.at[i])
-        for i, (src, dst) in enumerate(((wk_hbm, wk), (wv_hbm, wv), (wq_hbm, wq)))
+        for i, (src, dst) in enumerate((
+            (kv_hbm, kv_ref), (q_hbm, q_ref), (wk_hbm, wk), (wv_hbm, wv), (do_hbm, do_ref), (wq_hbm, wq),
+        ))
     ]
     for load in loads:
         load.start()
@@ -137,26 +139,31 @@
         )
         for c in range(CHUNKS)
     ]
+    loads[0].wait()
     kv_gather.start(0)
+    pass_on(me, kv_ref)
+    loads[1].wait()
     q_gathers[0].start(0)
-    pass_on(me, kv_ref)
     kv_in[me] = kv_ref[...]
+    for c in range(1, CHUNKS):
+        q_in[c, me] = q_ref[c * part_rows:(c + 1) * part_rows, :]
 
     key_pos = lax.broadcasted_iota(jnp.int32, (part_rows, part_rows), 1)
     query_pos = lax.broadcasted_iota(jnp.int32, (part_rows, part_rows), 0)
     bias[...] = jnp.where(key_pos <= query_pos, F32(0.0), F32(-1e30))
     prev_mask = jnp.where(ctx == 0, F32(-1e30), F32(0.0))
-    for c in range(CHUNKS - 1):
-        seen = rows + (c + 1) * part_rows
-        unseen = jnp.zeros((heads, part_rows, 2 * rows - seen), BF16)
-        pb_all[:, c * part_rows:(c + 1) * part_rows, seen:] = unseen
-        ds_all[:, c * part_rows:(c + 1) * part_rows, seen:] = unseen
+    def clear_unseen():
+        for c in range(CHUNKS - 1):
+            seen = rows + (c + 1) * part_rows
+            unseen = jnp.zeros((heads, part_rows, 2 * rows - seen), BF16)
+            pb_all[:, c * part_rows:(c + 1) * part_rows, seen:] = unseen
+            ds_all[:, c * part_rows:(c + 1) * part_rows, seen:] = unseen
 
     def turn(src, dst):
-        @pl.loop(0, heads // 2)
+        @pl.loop(0, heads // 4)
         def _(j):
-            for u in range(2):
-                at = pl.multiple_of((2 * j + u) * NOPE, NOPE)
+            for u in range(4):
+                at = pl.multiple_of((4 * j + u) * NOPE, NOPE)
                 dst[pl.ds(at, NOPE), :] = src[:, pl.ds(at, NOPE)].T
 
     def kv_step(t):
@@ -167,7 +174,7 @@
 
     def add_queries(c, block, owner, first=False):
         at = pl.multiple_of(owner * q_cols, q_cols)
-        tile = 4 * WIDTH
+        tile = 8 * WIDTH
 
         @pl.loop(0, wq.shape[1] // tile)
         def _(j):
@@ -186,6 +193,20 @@
 
     def finish_queries(c):
         q_b[c * part_rows:(c + 1) * part_rows, :] = q_acc[...].astype(BF16)
+
+    def all_queries(c):
+        tile = 4 * WIDTH
+
+        @pl.loop(0, wq.shape[1] // tile)
+        def _(j):
+            cols = pl.ds(pl.multiple_of(j * tile, tile), tile)
+            if q_cols % 128 == 0:
+                total = nn(jnp.concatenate([q_in[c, i] for i in range(n_head)], 1), wq[:, cols])
+            else:
+                total = nn(q_in[c, 0], wq[:q_cols, cols])
+                for i in range(1, n_head):
+                    total += nn(q_in[c, i], wq[i * q_cols:(i + 1) * q_cols, cols])
+            q_b[c * part_rows:(c + 1) * part_rows, cols] = total.astype(BF16)
 
     def assemble(parts, row):
         span = slice(row, row + rows)
@@ -238,24 +259,24 @@
         query = q_b[span_of(c), window(h, odd)]
         key = [keys_t[columns(h), :seen], lat_t[KVL:, :seen]]
         pad = [jnp.zeros((ROPE, seen), BF16)]
-        s_buf[:, :seen] = nn(query, jnp.concatenate(pad + key if odd else key + pad, 0))
-
-    def softmax_stage(c, h):
+        s_buf[odd, :, :seen] = nn(query, jnp.concatenate(pad + key if odd else key + pad, 0))
+
+    def softmax_stage(c, h, odd):
         seen = seen_by(c)
-        dp_buf[:, :seen] = nn(do_ref[span_of(c), columns(h)], values_t[columns(h), :seen])
+        dp_buf[odd, :, :seen] = nn(do_ref[span_of(c), columns(h)], values_t[columns(h), :seen])
         for sub, row in pieces(c):
-            scores = [s_buf[sub, :rows] + prev_mask]
+            scores = [s_buf[odd, sub, :rows] + prev_mask]
             if c > 0:
-                scores.append(s_buf[sub, rows:seen - part_rows])
-            scores.append(s_buf[sub, seen - part_rows:seen] + bias[sub, :])
+                scores.append(s_buf[odd, sub, rows:seen - part_rows])
+            scores.append(s_buf[odd, sub, seen - part_rows:seen] + bias[sub, :])
             scores = jnp.concatenate(scores, 1)
             top = jnp.max(scores, 1, keepdims=True)
             expons = jnp.exp2((scores - top) * F32(SCALE * math.log2(math.e)))
             probs = expons * (F32(1.0) / jnp.sum(expons, 1, keepdims=True))
-            p_buf[sub, :seen] = probs
+            p_buf[odd, sub, :seen] = probs
             pb_all[h, row, :seen] = probs.astype(BF16)
 
-    def output_stage(c, h):
+    def output_stage(c, h, odd):
         seen = seen_by(c)
         span = span_of(c)
         cols = columns(h)
@@ -263,7 +284,7 @@
         out_ref[span, cols] = result
         row_dot = jnp.sum(do_ref[span, cols].astype(F32) * result.astype(F32), 1, keepdims=True)
         for sub, row in pieces(c):
-            dscore = p_buf[sub, :seen] * (dp_buf[sub, :seen] - row_dot[sub]) * F32(SCALE)
+            dscore = p_buf[odd, sub, :seen] * (dp_buf[odd, sub, :seen] - row_dot[sub]) * F32(SCALE)
             ds_all[h, row, :seen] = dscore.astype(BF16)
 
     def gradient_stage(c, h, odd, valid):
@@ -291,20 +312,24 @@
         def _(t):
             for i, hook in enumerate(hooks):
                 pl.when(t == trips * (i + 1) // count)(hook)
-            for u in range(2):
-                odd = u == 1
-                step = 2 * t + u
-                gradient_stage(c, jnp.maximum(step - 3, 0 if odd else 1), not odd, step >= 3)
-                output_stage(c, jnp.maximum(step - 2, 0))
-                softmax_stage(c, jnp.maximum(step - 1, 0))
-                score_stage(c, step, odd)
-
-        gradient_stage(c, heads - 3, True, None)
-        output_stage(c, heads - 2)
-        softmax_stage(c, heads - 1)
-        gradient_stage(c, heads - 2, False, None)
-        output_stage(c, heads - 1)
-        gradient_stage(c, heads - 1, True, None)
+            for odd in range(2):
+                gradient_stage(c, 2 * jnp.maximum(t - 3, 0) + odd, odd, t >= 3)
+            for odd in range(2):
+                output_stage(c, 2 * jnp.maximum(t - 2, 0) + odd, odd)
+            for odd in range(2):
+                softmax_stage(c, 2 * jnp.maximum(t - 1, 0) + odd, odd)
+            for odd in range(2):
+                score_stage(c, 2 * t + odd, odd)
+
+        for t in range(trips, trips + 3):
+            for odd in range(2):
+                gradient_stage(c, 2 * (t - 3) + odd, odd, None)
+            for odd in range(2):
+                if t < trips + 2:
+                    output_stage(c, 2 * (t - 2) + odd, odd)
+            for odd in range(2):
+                if t < trips + 1:
+                    softmax_stage(c, 2 * (t - 1) + odd, odd)
 
     class Reduce:
         def __init__(self, part, out, in_right, in_left, send, recv_right, recv_left, stages):
@@ -331,8 +356,11 @@
                     self.out(owner)[...] = stage[...].astype(BF16)
                     copy_of(self.out(owner), slots(owner), self.send(owner), recv(owner), device).start()
 
-        def total(self, stage):
-            stage[...] = self.part(me)
+        def total(self, stage, begin=True, end=True):
+            if begin:
+                stage[...] = self.part(me)
+            if not end:
+                return
             for slots, recv, device, _, joined in self.ways:
                 @pl.when(joined)
                 def _():
@@ -381,28 +409,31 @@
         kv_stage,
     )
 
-    loads[0].wait()
+    loads[2].wait()
     turn(wk, wkt)
     if last > 0:
         kv_step(0)
-    loads[1].wait()
+    loads[3].wait()
     turn(wv, wvt)
+    clear_unseen()
+    loads[4].wait()
+    turn(do_ref, dot_t)
     if last > 0:
         q_step(0, 0)
-    turn(do_ref, dot_t)
+    loads[5].wait()
+    own_queries(0)
     for t in range(1, last - 1):
         kv_step(t)
-    loads[2].wait()
-    own_queries(0)
-    for t in range(1, last):
         add_arrived(0, t - 1)
         q_step(0, t)
-        if t == max(1, last - 2):
-            q_gathers[1].start(0)
+    q_gathers[1].start(0)
     if last > 1:
+        add_arrived(0, last - 2)
         kv_step(last - 1)
     assemble([kv_in[i] for i in range(n_head)], rows)
     expand(rows)
+    if last > 1:
+        q_step(0, last - 1)
     for i in range(n_head):
         copy_of(kv_ref, kv_prev.at[i], p_send.at[i], p_recv.at[i], after).wait_recv()
     assemble([kv_prev[i] for i in range(n_head)], 0)
@@ -416,15 +447,16 @@
     attention(0, [functools.partial(q_step, 1, t) for t in range(1, last)])
     if last > 0:
         q_reduces[0].step(0)
-    own_queries(1)
-    for t in range(last):
-        add_arrived(1, t)
-    finish_queries(1)
+    all_queries(1)
     attention(1, [functools.partial(q_reduces[0].step, t) for t in range(1, last)])
 
     def project(row):
         span = slice(row, row + rows)
         return nn(wk[...], gk_t[:, span]) + nn(wv[...], gv_t[:, span])
+
+    def finish_chunk(c, stage, begin=True):
+        q_reduces[c].total(stage, begin)
+        gq_ref[span_of(c), :] = stage[...].T
 
     final = q_reduces[1]
     if last > 0:
@@ -437,18 +469,19 @@
         final.step(1)
     gkv_own[:KVL, :] = project(rows)
     gkv_own[KVL:, :] = krope[:, rows:]
-    if last > 2:
-        final.step(2)
+    for t in range(2, last):
+        final.step(t)
     back.wait_recv()
     gkv_own[...] += back_in[...].astype(F32)
-    for t in range(last):
+    if last > 0:
+        kv_reduce.step(0)
+    finish_chunk(0, stage_own)
+    if last > 1:
+        kv_reduce.step(1)
+    final.total(stage_own, end=False)
+    for t in range(2, last):
         kv_reduce.step(t)
-        if t + 3 < last:
-            final.step(t + 3)
-
-    for c in range(CHUNKS):
-        q_reduces[c].total(stage_right)
-        gq_ref[:, c * part_rows:(c + 1) * part_rows] = stage_right[...]
+    finish_chunk(1, stage_own, False)
     kv_reduce.total(gkv_ref)
 
     kv_gather.finish()
@@ -463,6 +496,15 @@
 
 CHUNKS = 2
 PIECE = 32
+
+
+def store(*refs):
+    sems = refs[6]
+    copies = [pltpu.make_async_copy(refs[i], refs[i + 3], sems.at[i]) for i in range(3)]
+    for copy in copies:
+        copy.start()
+    for copy in copies:
+        copy.wait()
 
 
 def on_device(n_ctx, n_head, q_latent, kv_latent, w_query, w_key, w_value, d_out):
@@ -478,16 +520,20 @@
     dma = pltpu.SemaphoreType.DMA
     some = (n_head,)
     each = (CHUNKS, n_head)
-    out, gq_t, gkv_t = pl.pallas_call(
+    results = (
+        ((rows, kw), BF16),
+        ((rows, q_cols), F32),
+        ((kv_cols, rows), F32),
+    )
+    parts = pl.pallas_call(
         functools.partial(kernel, n_ctx, n_head),
-        out_shape=(
-            jax.ShapeDtypeStruct((rows, kw), BF16),
-            jax.ShapeDtypeStruct((q_cols, rows), F32),
-            jax.ShapeDtypeStruct((kv_cols, rows), F32),
-        ),
-        in_specs=[vmem, vmem, vmem, hbm, hbm, hbm],
+        out_shape=tuple(pltpu.VMEM(shape, dtype) for shape, dtype in results),
+        in_specs=[hbm] * 6,
         out_specs=(vmem, vmem, vmem),
         scratch_shapes=[
+            pltpu.VMEM((rows, q_cols), BF16),
+            pltpu.VMEM((kv_cols, rows), BF16),
+            pltpu.VMEM((rows, kw), BF16),
             pltpu.VMEM((ql, qw), BF16),
             pltpu.VMEM((KVL, kw), BF16),
             pltpu.VMEM((KVL, kw), BF16),
@@ -502,9 +548,9 @@
             pltpu.VMEM((rows, qw), BF16),
             pltpu.VMEM((kw, 2 * rows), BF16),
             pltpu.VMEM((kw, 2 * rows), BF16),
-            pltpu.VMEM((part_rows, 2 * rows), F32),
-            pltpu.VMEM((part_rows, 2 * rows), F32),
-            pltpu.VMEM((part_rows, 2 * rows), F32),
+            pltpu.VMEM((2, part_rows, 2 * rows), F32),
+            pltpu.VMEM((2, part_rows, 2 * rows), F32),
+            pltpu.VMEM((2, part_rows, 2 * rows), F32),
             pltpu.VMEM((heads, rows, 2 * rows), BF16),
             pltpu.VMEM((heads, rows, 2 * rows), BF16),
             pltpu.VMEM((qw, rows), BF16),
@@ -522,8 +568,9 @@
             pltpu.VMEM((kvw, rows), F32),
             pltpu.VMEM((q_cols, part_rows), F32),
             pltpu.VMEM((q_cols, part_rows), F32),
+            pltpu.VMEM((q_cols, part_rows), F32),
             pltpu.VMEM((part_rows, part_rows), F32),
-            dma((3,)),
+            dma((6,)),
             dma(some), dma(some), dma(some),
             dma(each), dma(each), dma(each),
             dma(some), dma(some),
@@ -532,11 +579,19 @@
             dma(some), dma(some), dma(some),
         ],
         compiler_params=pltpu.CompilerParams(
-            collective_id=0, has_side_effects=True, vmem_limit_bytes=62 * 1024 * 1024,
+            collective_id=0, has_side_effects=True, vmem_limit_bytes=58 * 1024 * 1024,
         ),
         name="latent_attention",
     )(q_latent, kv_latent.T, d_out, w_query, w_key, w_value)
-    return out, gq_t.T, gkv_t.T
+    out, gq, gkv_t = pl.pallas_call(
+        store,
+        out_shape=tuple(jax.ShapeDtypeStruct(shape, dtype) for shape, dtype in results),
+        in_specs=[vmem] * 3,
+        out_specs=(hbm,) * 3,
+        scratch_shapes=[dma((3,))],
+        name="store_results",
+    )(*(pltpu.with_memory_space_constraint(part, pltpu.VMEM) for part in parts))
+    return out, gq, gkv_t.T
 
 
 def solution(mesh):

time: 74 us -> 61.3 us (0.83)
  Pallas kernels: 68.2 us -> 60.4 us
  local copies, waits for them, and re-layouts: 4.91 us -> 0 us
    pallas_call x1 -> x2, Pallas kernels: 68.2 us -> 60.4 us  [the longest x1 59.2 us: on_device(): pl.pallas_call(functools.partial(kernel, n_ctx, n_head), out_shape=tuple(...]
    unnamed x5 -> x0, local copies, waits for them, and re-layouts: 4.91 us -> none
where the time goes in v2:
time: 61.3 us; the launch traced here: 61.2 us
  Pallas kernels  60.4 us (99%)
  between operations  0.8 us (1%)
    pallas_call x1, Pallas kernels, on_device(): pl.pallas_call(functools.partial(kernel, n_ctx, n_head), out_shape=tuple(...  59.2 us

profile of v2, /device:TPU:0, one launch (start us, length us, event | category | flops | bytes accessed | tf_op | source)
XLA Modules:
  0.0 61.2 jit_solution(11790341433584050488)
XLA Ops:
  0.6 59.2 %latent_attention.1 = (bf16[256,2048]{1,0:T(8,128)(2,1)S(1)}, f32[256,384]{1,0:T(8,128)S(1)}, f32[144,256]{1,0:T(8,128)S(1)}) custom-call(bf16[256,384]{1,0:T(8,128)(2,1)} %q_hbm.1, bf16[144,256]{1,0:T(8,128)(2,1)} %bitcast.2, bf16[256,2048]{1,0:T(8,128)(2,1)} %do_hbm.1, bf16[1536,3072]{1,0:T(8,128)(2,1)} %wq_hbm.1, bf16[512,2048]{1,0:T(8,128)(2,1)} %wk_hbm.1, ...), custom_call_target="tpu_custom_call" | custom-call | tf_op jit(solution)/shard_map/latent_attention/pallas_call | solution.py:528
  59.9 1.2 %store_results.1 = (bf16[256,2048]{1,0:T(8,128)(2,1)}, f32[256,384]{1,0:T(8,128)}, f32[144,256]{1,0:T(8,128)}) custom-call(bf16[256,2048]{1,0:T(8,128)(2,1)S(1)} %get-tuple-element.9.refs_0_, f32[256,384]{1,0:T(8,128)S(1)} %get-tuple-element.10.refs_1_, f32[144,256]{1,0:T(8,128)S(1)} %get-tuple-element.11.refs_2_), custom_call_target="tpu_custom_call" | custom-call | tf_op jit(solution)/shard_map/store_results/pallas_call | solution.py:586

commit v3 on v2

--- a/solution.py
+++ b/solution.py
@@ -174,7 +174,7 @@
 
     def add_queries(c, block, owner, first=False):
         at = pl.multiple_of(owner * q_cols, q_cols)
-        tile = 8 * WIDTH
+        tile = heads * WIDTH
 
         @pl.loop(0, wq.shape[1] // tile)
         def _(j):
@@ -195,7 +195,7 @@
         q_b[c * part_rows:(c + 1) * part_rows, :] = q_acc[...].astype(BF16)
 
     def all_queries(c):
-        tile = 4 * WIDTH
+        tile = 8 * WIDTH
 
         @pl.loop(0, wq.shape[1] // tile)
         def _(j):
@@ -225,10 +225,10 @@
         lat_t[:, span] = total.astype(BF16)
 
     def expand(row):
-        tile = 4 * NOPE
+        tile = 8 * NOPE
         span = slice(row, row + rows)
 
-        @pl.loop(0, heads // 4)
+        @pl.loop(0, heads // 8)
         def _(j):
             cols = pl.ds(pl.multiple_of(j * tile, tile), tile)
             main_t = lat_t[:KVL, span]
@@ -287,7 +287,7 @@
             dscore = p_buf[odd, sub, :seen] * (dp_buf[odd, sub, :seen] - row_dot[sub]) * F32(SCALE)
             ds_all[h, row, :seen] = dscore.astype(BF16)
 
-    def gradient_stage(c, h, odd, valid):
+    def gradient_stage(c, h, odd):
         seen = seen_by(c)
         span = span_of(c)
         cols = columns(h)
@@ -300,36 +300,39 @@
         query_t = query_t[ROPE:] if odd else query_t[:WIDTH]
         g_key = nn(query_t, ds_all[h])
         gk_t[cols, :] = g_key[:NOPE].astype(BF16)
-        g_rope = g_key[NOPE:].astype(BF16).astype(F32)
-        krope[...] += g_rope if valid is None else jnp.where(valid, g_rope, F32(0.0))
+        krope[...] += g_key[NOPE:].astype(BF16).astype(F32)
         gv_t[cols, :] = nn(dot_t[cols, :], pb_all[h]).astype(BF16)
 
     def attention(c, hooks):
         trips = heads // 2
-        count = len(hooks) + 1
-
-        @pl.loop(0, trips)
+
+        def trip(t, stages):
+            if "g" in stages:
+                for odd in range(2):
+                    gradient_stage(c, 2 * (t - 3) + odd, odd)
+            if "o" in stages:
+                for odd in range(2):
+                    output_stage(c, 2 * (t - 2) + odd, odd)
+            if "p" in stages:
+                for odd in range(2):
+                    softmax_stage(c, 2 * (t - 1) + odd, odd)
+            if "s" in stages:
+                for odd in range(2):
+                    score_stage(c, 2 * t + odd, odd)
+
+        trip(0, "s")
+        trip(1, "ps")
+        trip(2, "ops")
+
+        @pl.loop(3, trips)
         def _(t):
             for i, hook in enumerate(hooks):
-                pl.when(t == trips * (i + 1) // count)(hook)
-            for odd in range(2):
-                gradient_stage(c, 2 * jnp.maximum(t - 3, 0) + odd, odd, t >= 3)
-            for odd in range(2):
-                output_stage(c, 2 * jnp.maximum(t - 2, 0) + odd, odd)
-            for odd in range(2):
-                softmax_stage(c, 2 * jnp.maximum(t - 1, 0) + odd, odd)
-            for odd in range(2):
-                score_stage(c, 2 * t + odd, odd)
-
-        for t in range(trips, trips + 3):
-            for odd in range(2):
-                gradient_stage(c, 2 * (t - 3) + odd, odd, None)
-            for odd in range(2):
-                if t < trips + 2:
-                    output_stage(c, 2 * (t - 2) + odd, odd)
-            for odd in range(2):
-                if t < trips + 1:
-                    softmax_stage(c, 2 * (t - 1) + odd, odd)
+                pl.when(t == 3 + ((trips - 3) * (2 * i + 1)) // (2 * len(hooks)))(hook)
+            trip(t, "gops")
+
+        trip(trips, "gop")
+        trip(trips + 1, "go")
+        trip(trips + 2, "g")
 
     class Reduce:
         def __init__(self, part, out, in_right, in_left, send, recv_right, recv_left, stages):
@@ -381,8 +384,11 @@
 
         return part
 
-    def kv_part(owner):
-        return gkv_own[pl.ds(pl.multiple_of(owner * kv_cols, 8), kv_cols), :]
+    def kv_part(c):
+        def part(owner):
+            return gkv_own[pl.ds(pl.multiple_of(owner * kv_cols, 8), kv_cols), span_of(c)]
+
+        return part
 
     q_reduces = [
         Reduce(
@@ -397,17 +403,19 @@
         )
         for c in range(CHUNKS)
     ]
-    kv_stage = (gkv_ref, gkv_ref)
-    kv_reduce = Reduce(
-        kv_part,
-        lambda i: rkv_out.at[i],
-        lambda i: rkv_right.at[i],
-        lambda i: rkv_left.at[i],
-        lambda i: rkv_send.at[i],
-        lambda i: rkv_rr.at[i],
-        lambda i: rkv_rl.at[i],
-        kv_stage,
-    )
+    kv_reduces = [
+        Reduce(
+            kv_part(c),
+            lambda i, c=c: rkv_out.at[c, i],
+            lambda i, c=c: rkv_right.at[c, i],
+            lambda i, c=c: rkv_left.at[c, i],
+            lambda i, c=c: rkv_send.at[c, i],
+            lambda i, c=c: rkv_rr.at[c, i],
+            lambda i, c=c: rkv_rl.at[c, i],
+            (gkv_ref.at[:, span_of(c)],) * 2,
+        )
+        for c in range(CHUNKS)
+    ]
 
     loads[2].wait()
     turn(wk, wkt)
@@ -416,6 +424,7 @@
     loads[3].wait()
     turn(wv, wvt)
     clear_unseen()
+    krope[...] = jnp.zeros_like(krope)
     loads[4].wait()
     turn(do_ref, dot_t)
     if last > 0:
@@ -439,14 +448,14 @@
     assemble([kv_prev[i] for i in range(n_head)], 0)
     expand(0)
     if last > 0:
+        q_step(1, 0)
         add_arrived(0, last - 1)
     finish_queries(0)
-    krope[...] = jnp.zeros_like(krope)
-    if last > 0:
-        q_step(1, 0)
-    attention(0, [functools.partial(q_step, 1, t) for t in range(1, last)])
+    attention(0, [functools.partial(q_step, 1, t) for t in range(1, last - 1)])
     if last > 0:
         q_reduces[0].step(0)
+    if last > 1:
+        q_step(1, last - 1)
     all_queries(1)
     attention(1, [functools.partial(q_reduces[0].step, t) for t in range(1, last)])
 
@@ -471,22 +480,20 @@
     gkv_own[KVL:, :] = krope[:, rows:]
     for t in range(2, last):
         final.step(t)
+    finish_chunk(0, stage_own)
+    final.total(stage_own, end=False)
     back.wait_recv()
     gkv_own[...] += back_in[...].astype(F32)
-    if last > 0:
-        kv_reduce.step(0)
-    finish_chunk(0, stage_own)
-    if last > 1:
-        kv_reduce.step(1)
-    final.total(stage_own, end=False)
-    for t in range(2, last):
-        kv_reduce.step(t)
+    for t in range(last):
+        for c in range(CHUNKS):
+            kv_reduces[c].step(t)
     finish_chunk(1, stage_own, False)
-    kv_reduce.total(gkv_ref)
+    for c in range(CHUNKS):
+        kv_reduces[c].total(gkv_ref.at[:, span_of(c)])
 
     kv_gather.finish()
-    kv_reduce.finish()
     for c in range(CHUNKS):
+        kv_reduces[c].finish()
         q_gathers[c].finish()
         q_reduces[c].finish()
     for i in range(n_head):
@@ -562,9 +569,9 @@
             pltpu.VMEM((CHUNKS, n_head, q_cols, part_rows), BF16),
             pltpu.VMEM((CHUNKS, n_head, q_cols, part_rows), BF16),
             pltpu.VMEM((CHUNKS, n_head, q_cols, part_rows), BF16),
-            pltpu.VMEM((n_head, kv_cols, rows), BF16),
-            pltpu.VMEM((n_head, kv_cols, rows), BF16),
-            pltpu.VMEM((n_head, kv_cols, rows), BF16),
+            pltpu.VMEM((CHUNKS, n_head, kv_cols, part_rows), BF16),
+            pltpu.VMEM((CHUNKS, n_head, kv_cols, part_rows), BF16),
+            pltpu.VMEM((CHUNKS, n_head, kv_cols, part_rows), BF16),
             pltpu.VMEM((kvw, rows), F32),
             pltpu.VMEM((q_cols, part_rows), F32),
             pltpu.VMEM((q_cols, part_rows), F32),
@@ -576,7 +583,7 @@
             dma(some), dma(some),
             dma, dma,
             dma(each), dma(each), dma(each),
-            dma(some), dma(some), dma(some),
+            dma(each), dma(each), dma(each),
         ],
         compiler_params=pltpu.CompilerParams(
             collective_id=0, has_side_effects=True, vmem_limit_bytes=58 * 1024 * 1024,

time: 61.3 us -> 58.5 us (0.954)
  Pallas kernels: 60.4 us -> 57.6 us
    pallas_call x1, Pallas kernels: 59.2 us -> 56.4 us  [on_device(): pl.pallas_call(functools.partial(kernel, n_ctx, n_head), out_shape=tuple(...]
where the time goes in v3:
time: 58.5 us; the launch traced here: 58.4 us
  Pallas kernels  57.6 us (98%)
  between operations  0.8 us (1%)
    pallas_call x1, Pallas kernels, on_device(): pl.pallas_call(functools.partial(kernel, n_ctx, n_head), out_shape=tuple(...  56.4 us

profile of v3, /device:TPU:0, one launch (start us, length us, event | category | flops | bytes accessed | tf_op | source)
XLA Modules:
  0.0 58.4 jit_solution(696461875301471658)
XLA Ops:
  0.6 56.4 %latent_attention.1 = (bf16[256,2048]{1,0:T(8,128)(2,1)S(1)}, f32[256,384]{1,0:T(8,128)S(1)}, f32[144,256]{1,0:T(8,128)S(1)}) custom-call(bf16[256,384]{1,0:T(8,128)(2,1)} %q_hbm.1, bf16[144,256]{1,0:T(8,128)(2,1)} %bitcast.2, bf16[256,2048]{1,0:T(8,128)(2,1)} %do_hbm.1, bf16[1536,3072]{1,0:T(8,128)(2,1)} %wq_hbm.1, bf16[512,2048]{1,0:T(8,128)(2,1)} %wk_hbm.1, ...), custom_call_target="tpu_custom_call" | custom-call | tf_op jit(solution)/shard_map/latent_attention/pallas_call | solution.py:535
  57.0 1.2 %store_results.1 = (bf16[256,2048]{1,0:T(8,128)(2,1)}, f32[256,384]{1,0:T(8,128)}, f32[144,256]{1,0:T(8,128)}) custom-call(bf16[256,2048]{1,0:T(8,128)(2,1)S(1)} %get-tuple-element.9.refs_0_, f32[256,384]{1,0:T(8,128)S(1)} %get-tuple-element.10.refs_1_, f32[144,256]{1,0:T(8,128)S(1)} %get-tuple-element.11.refs_2_), custom_call_target="tpu_custom_call" | custom-call | tf_op jit(solution)/shard_map/store_results/pallas_call | solution.py:593

commit v4 on v3

--- a/solution.py
+++ b/solution.py
@@ -33,7 +33,7 @@
     out_ref, gq_ref, gkv_ref,
     q_ref, kv_ref, do_ref, wq, wk, wv, wkt, wvt, dot_t, q_in, kv_in, kv_prev, lat_t, q_acc, q_b,
     keys_t, values_t, s_buf, dp_buf, p_buf, pb_all, ds_all, gq_t, gk_t, gv_t, krope, back_out, back_in,
-    rq_out, rq_right, rq_left, rkv_out, rkv_right, rkv_left, gkv_own, stage_right, stage_left, stage_own,
+    rq_out, rq_right, rq_left, rkv_out, rkv_right, rkv_left, gkv_own, stage_right, stage_own,
     bias, w_sem, kv_r, kv_l, kv_recv, q_r, q_l, q_recv, p_send, p_recv,
     b_send, b_recv, rq_send, rq_rr, rq_rl, rkv_send, rkv_rr, rkv_rl,
 ):
@@ -62,17 +62,14 @@
 
     barrier = pltpu.get_barrier_semaphore()
 
-    @pl.when(has_right)
-    def _():
-        pl.semaphore_signal(barrier, inc=1, device_id=right, device_id_type=MESH)
-
-    @pl.when(has_left)
-    def _():
-        pl.semaphore_signal(barrier, inc=1, device_id=left, device_id_type=MESH)
+    for peer in range(n_head):
+        @pl.when(me != peer)
+        def _():
+            pl.semaphore_signal(barrier, inc=1, device_id={"head": peer}, device_id_type=MESH)
 
     pl.semaphore_signal(barrier, inc=1, device_id=after, device_id_type=MESH)
     pl.semaphore_signal(barrier, inc=1, device_id=before, device_id_type=MESH)
-    pl.semaphore_wait(barrier, 2 + jnp.minimum(me, 1) + jnp.minimum(last - me, 1))
+    pl.semaphore_wait(barrier, 2 + last)
 
     def copy_of(src, dst, send_sem, recv_sem, device):
         return pltpu.make_async_remote_copy(
@@ -287,21 +284,24 @@
             dscore = p_buf[odd, sub, :seen] * (dp_buf[odd, sub, :seen] - row_dot[sub]) * F32(SCALE)
             ds_all[h, row, :seen] = dscore.astype(BF16)
 
-    def gradient_stage(c, h, odd):
+    def value_gradient(c, h):
+        if c + 1 == CHUNKS:
+            gv_t[columns(h), :] = nn(dot_t[columns(h), :], pb_all[h]).astype(BF16)
+
+    def key_gradient(c, h, odd):
+        if c + 1 == CHUNKS:
+            query_t = q_b[:, window(h, odd)].T
+            query_t = query_t[ROPE:] if odd else query_t[:WIDTH]
+            g_key = nn(query_t, ds_all[h])
+            gk_t[columns(h), :] = g_key[:NOPE].astype(BF16)
+            krope[...] += g_key[NOPE:].astype(BF16).astype(F32)
+
+    def query_gradient(c, h):
         seen = seen_by(c)
         span = span_of(c)
-        cols = columns(h)
-        key = jnp.concatenate([keys_t[cols, :seen], lat_t[KVL:, :seen]], 0)
+        key = jnp.concatenate([keys_t[columns(h), :seen], lat_t[KVL:, :seen]], 0)
         q_at = pl.ds(pl.multiple_of(h * WIDTH, ROPE), WIDTH)
         gq_t[q_at, span] = nt(key, ds_all[h, span, :seen]).astype(BF16)
-        if c + 1 < CHUNKS:
-            return
-        query_t = q_b[:, window(h, odd)].T
-        query_t = query_t[ROPE:] if odd else query_t[:WIDTH]
-        g_key = nn(query_t, ds_all[h])
-        gk_t[cols, :] = g_key[:NOPE].astype(BF16)
-        krope[...] += g_key[NOPE:].astype(BF16).astype(F32)
-        gv_t[cols, :] = nn(dot_t[cols, :], pb_all[h]).astype(BF16)
 
     def attention(c, hooks):
         trips = heads // 2
@@ -309,7 +309,11 @@
         def trip(t, stages):
             if "g" in stages:
                 for odd in range(2):
-                    gradient_stage(c, 2 * (t - 3) + odd, odd)
+                    value_gradient(c, 2 * (t - 3) + odd)
+                for odd in range(2):
+                    key_gradient(c, 2 * (t - 3) + odd, odd)
+                for odd in range(2):
+                    query_gradient(c, 2 * (t - 3) + odd)
             if "o" in stages:
                 for odd in range(2):
                     output_stage(c, 2 * (t - 2) + odd, odd)
@@ -335,40 +339,58 @@
         trip(trips + 2, "g")
 
     class Reduce:
-        def __init__(self, part, out, in_right, in_left, send, recv_right, recv_left, stages):
-            self.part, self.out, self.send = part, out, send
-            self.ways = (
-                (in_right, recv_right, right, stages[0], has_left),
-                (in_left, recv_left, left, stages[1], has_right),
-            )
-
-        def step(self, tick):
-            for way, (slots, recv, device, stage, joined) in enumerate(self.ways):
-                lag = me if way == 0 else last - me
-                owner = last - (tick - lag) if way == 0 else tick - lag
-
-                @pl.when(tick >= lag)
-                def _():
-                    stage[...] = self.part(owner)
-
-                    @pl.when(joined)
-                    def _():
-                        copy_of(slots(owner), slots(owner), self.send(owner), recv(owner), device).wait_recv()
-                        stage[...] += slots(owner)[...].astype(F32)
-
-                    self.out(owner)[...] = stage[...].astype(BF16)
-                    copy_of(self.out(owner), slots(owner), self.send(owner), recv(owner), device).start()
+        def __init__(self, part, out, relay, final, send, relay_recv, final_recv, stage):
+            self.part, self.out, self.relay, self.final = part, out, relay, final
+            self.send, self.relay_recv, self.final_recv, self.stage = send, relay_recv, final_recv, stage
+
+        def step(self, t):
+            adds_left = lax.rem(last - me, 2) == 1
+            adds_right = lax.rem(me, 2) == 1
+            left_first = jnp.logical_or(jnp.logical_not(adds_left), adds_right)
+            first = jnp.where(left_first, me, last - me)
+            in_first = t < first
+            at = jnp.where(in_first, t, t - first)
+            on_left = in_first == left_first
+            owner = jnp.where(on_left, at, last - at)
+            adds = jnp.where(on_left, adds_left, adds_right)
+            outer = jnp.logical_and(jnp.logical_not(adds), jnp.abs(me - owner) > 1)
+            stage = self.stage
+            stage[...] = self.part(owner)
+            out = self.out(owner)
+
+            def send_to(slot, recv, device):
+                return copy_of(out, slot, self.send(owner), recv, {"head": device})
+
+            @pl.when(adds)
+            def _():
+                slot = self.relay(owner)
+                copy_of(slot, slot, self.send(owner), self.relay_recv(owner), right).wait_recv()
+                stage[...] += slot[...].astype(F32)
+
+            out[...] = stage[...].astype(BF16)
+
+            @pl.when(outer)
+            def _():
+                send_to(self.relay(owner), self.relay_recv(owner), jnp.where(on_left, me - 1, me + 1)).start()
+
+            @pl.when(jnp.logical_not(outer))
+            def _():
+                send_to(self.final(me), self.final_recv(me), owner).start()
 
         def total(self, stage, begin=True, end=True):
             if begin:
                 stage[...] = self.part(me)
             if not end:
                 return
-            for slots, recv, device, _, joined in self.ways:
-                @pl.when(joined)
+            for i in range(n_head):
+                from_right = (me < i) & ((me == i - 1) if (last - i) % 2 == 0 else (me < i))
+                from_left = (me > i) & ((me == i + 1) if i % 2 == 0 else (me > i))
+
+                @pl.when(from_right | from_left)
                 def _():
-                    copy_of(slots(me), slots(me), self.send(me), recv(me), device).wait_recv()
-                    stage[...] += slots(me)[...].astype(F32)
+                    slot = self.final(i)
+                    copy_of(slot, slot, self.send(i), self.final_recv(i), right).wait_recv()
+                    stage[...] += slot[...].astype(F32)
 
         def finish(self):
             for i in range(n_head):
@@ -399,7 +421,7 @@
             lambda i, c=c: rq_send.at[c, i],
             lambda i, c=c: rq_rr.at[c, i],
             lambda i, c=c: rq_rl.at[c, i],
-            (stage_right, stage_left),
+            stage_right,
         )
         for c in range(CHUNKS)
     ]
@@ -412,7 +434,7 @@
             lambda i, c=c: rkv_send.at[c, i],
             lambda i, c=c: rkv_rr.at[c, i],
             lambda i, c=c: rkv_rl.at[c, i],
-            (gkv_ref.at[:, span_of(c)],) * 2,
+            gkv_ref.at[:, span_of(c)],
         )
         for c in range(CHUNKS)
     ]
@@ -433,9 +455,10 @@
     own_queries(0)
     for t in range(1, last - 1):
         kv_step(t)
+        if t == max(1, last - 2):
+            q_gathers[1].start(0)
         add_arrived(0, t - 1)
         q_step(0, t)
-    q_gathers[1].start(0)
     if last > 1:
         add_arrived(0, last - 2)
         kv_step(last - 1)
@@ -480,13 +503,16 @@
     gkv_own[KVL:, :] = krope[:, rows:]
     for t in range(2, last):
         final.step(t)
-    finish_chunk(0, stage_own)
-    final.total(stage_own, end=False)
     back.wait_recv()
     gkv_own[...] += back_in[...].astype(F32)
+    between = [lambda: finish_chunk(0, stage_own), lambda: final.total(stage_own, end=False)]
     for t in range(last):
         for c in range(CHUNKS):
             kv_reduces[c].step(t)
+        if between:
+            between.pop(0)()
+    for act in between:
+        act()
     finish_chunk(1, stage_own, False)
     for c in range(CHUNKS):
         kv_reduces[c].total(gkv_ref.at[:, span_of(c)])
@@ -575,7 +601,6 @@
             pltpu.VMEM((kvw, rows), F32),
             pltpu.VMEM((q_cols, part_rows), F32),
             pltpu.VMEM((q_cols, part_rows), F32),
-            pltpu.VMEM((q_cols, part_rows), F32),
             pltpu.VMEM((part_rows, part_rows), F32),
             dma((6,)),
             dma(some), dma(some), dma(some),

time: 58.5 us -> 56 us (0.957); the launches traced: 58.4 us -> 55.2 us
  Pallas kernels: 57.6 us -> 54.4 us
    pallas_call x1, Pallas kernels: 56.4 us -> 53.2 us  [on_device(): pl.pallas_call(functools.partial(kernel, n_ctx, n_head), out_shape=tuple(...]
where the time goes in v4:
time: 56 us; the launch traced here: 55.2 us
  Pallas kernels  54.4 us (97%)
  between operations  0.8 us (1%)
    pallas_call x1, Pallas kernels, on_device(): pl.pallas_call(functools.partial(kernel, n_ctx, n_head), out_shape=tuple(...  53.2 us
    pallas_call x1, Pallas kernels, on_device(): pl.pallas_call(store, out_shape=tuple((jax.ShapeDtypeStruct(shape, dtype)...  1.16 us

profile of v4, /device:TPU:0, one launch (start us, length us, event | category | flops | bytes accessed | tf_op | source)
XLA Modules:
  0.0 55.2 jit_solution(3693834503498398169)
XLA Ops:
  0.6 53.2 %latent_attention.1 = (bf16[256,2048]{1,0:T(8,128)(2,1)S(1)}, f32[256,384]{1,0:T(8,128)S(1)}, f32[144,256]{1,0:T(8,128)S(1)}) custom-call(bf16[256,384]{1,0:T(8,128)(2,1)} %q_hbm.1, bf16[144,256]{1,0:T(8,128)(2,1)} %bitcast.2, bf16[256,2048]{1,0:T(8,128)(2,1)} %do_hbm.1, bf16[1536,3072]{1,0:T(8,128)(2,1)} %wq_hbm.1, bf16[512,2048]{1,0:T(8,128)(2,1)} %wk_hbm.1, ...), custom_call_target="tpu_custom_call" | custom-call | tf_op jit(solution)/shard_map/latent_attention/pallas_call | solution.py:561
  53.8 1.2 %store_results.1 = (bf16[256,2048]{1,0:T(8,128)(2,1)}, f32[256,384]{1,0:T(8,128)}, f32[144,256]{1,0:T(8,128)}) custom-call(bf16[256,2048]{1,0:T(8,128)(2,1)S(1)} %get-tuple-element.9.refs_0_, f32[256,384]{1,0:T(8,128)S(1)} %get-tuple-element.10.refs_1_, f32[144,256]{1,0:T(8,128)S(1)} %get-tuple-element.11.refs_2_), custom_call_target="tpu_custom_call" | custom-call | tf_op jit(solution)/shard_map/store_results/pallas_call | solution.py:618

commit v5 on v4

--- a/solution.py
+++ b/solution.py
@@ -408,7 +408,7 @@
 
     def kv_part(c):
         def part(owner):
-            return gkv_own[pl.ds(pl.multiple_of(owner * kv_cols, 8), kv_cols), span_of(c)]
+            return gkv_own[pl.ds(pl.multiple_of(owner * kv_cols, 8), kv_cols), :]
 
         return part
 
@@ -434,9 +434,9 @@
             lambda i, c=c: rkv_send.at[c, i],
             lambda i, c=c: rkv_rr.at[c, i],
             lambda i, c=c: rkv_rl.at[c, i],
-            gkv_ref.at[:, span_of(c)],
+            gkv_ref,
         )
-        for c in range(CHUNKS)
+        for c in range(1)
     ]
 
     loads[2].wait()
@@ -507,19 +507,17 @@
     gkv_own[...] += back_in[...].astype(F32)
     between = [lambda: finish_chunk(0, stage_own), lambda: final.total(stage_own, end=False)]
     for t in range(last):
-        for c in range(CHUNKS):
-            kv_reduces[c].step(t)
+        kv_reduces[0].step(t)
         if between:
             between.pop(0)()
     for act in between:
         act()
     finish_chunk(1, stage_own, False)
+    kv_reduces[0].total(gkv_ref)
+
+    kv_gather.finish()
+    kv_reduces[0].finish()
     for c in range(CHUNKS):
-        kv_reduces[c].total(gkv_ref.at[:, span_of(c)])
-
-    kv_gather.finish()
-    for c in range(CHUNKS):
-        kv_reduces[c].finish()
         q_gathers[c].finish()
         q_reduces[c].finish()
     for i in range(n_head):
@@ -595,9 +593,9 @@
             pltpu.VMEM((CHUNKS, n_head, q_cols, part_rows), BF16),
             pltpu.VMEM((CHUNKS, n_head, q_cols, part_rows), BF16),
             pltpu.VMEM((CHUNKS, n_head, q_cols, part_rows), BF16),
-            pltpu.VMEM((CHUNKS, n_head, kv_cols, part_rows), BF16),
-            pltpu.VMEM((CHUNKS, n_head, kv_cols, part_rows), BF16),
-            pltpu.VMEM((CHUNKS, n_head, kv_cols, part_rows), BF16),
+            pltpu.VMEM((1, n_head, kv_cols, rows), BF16),
+            pltpu.VMEM((1, n_head, kv_cols, rows), BF16),
+            pltpu.VMEM((1, n_head, kv_cols, rows), BF16),
             pltpu.VMEM((kvw, rows), F32),
             pltpu.VMEM((q_cols, part_rows), F32),
             pltpu.VMEM((q_cols, part_rows), F32),

time: 56 us -> 56.7 us (1.012)
  no operation moved by 1% of the time
where the time goes in v5:
time: 56.7 us; the launch traced here: 55.5 us
  Pallas kernels  54.7 us (96%)
  between operations  0.8 us (1%)
    pallas_call x1, Pallas kernels, on_device(): pl.pallas_call(functools.partial(kernel, n_ctx, n_head), out_shape=tuple(...  53.6 us
    pallas_call x1, Pallas kernels, on_device(): pl.pallas_call(store, out_shape=tuple((jax.ShapeDtypeStruct(shape, dtype)...  1.16 us

profile of v5, /device:TPU:0, one launch (start us, length us, event | category | flops | bytes accessed | tf_op | source)
XLA Modules:
  0.0 55.5 jit_solution(17222725727477742274)
XLA Ops:
  0.6 53.6 %latent_attention.1 = (bf16[256,2048]{1,0:T(8,128)(2,1)S(1)}, f32[256,384]{1,0:T(8,128)S(1)}, f32[144,256]{1,0:T(8,128)S(1)}) custom-call(bf16[256,384]{1,0:T(8,128)(2,1)} %q_hbm.1, bf16[144,256]{1,0:T(8,128)(2,1)} %bitcast.2, bf16[256,2048]{1,0:T(8,128)(2,1)} %do_hbm.1, bf16[1536,3072]{1,0:T(8,128)(2,1)} %wq_hbm.1, bf16[512,2048]{1,0:T(8,128)(2,1)} %wk_hbm.1, ...), custom_call_target="tpu_custom_call" | custom-call | tf_op jit(solution)/shard_map/latent_attention/pallas_call | solution.py:559
  54.2 1.2 %store_results.1 = (bf16[256,2048]{1,0:T(8,128)(2,1)}, f32[256,384]{1,0:T(8,128)}, f32[144,256]{1,0:T(8,128)}) custom-call(bf16[256,2048]{1,0:T(8,128)(2,1)S(1)} %get-tuple-element.9.refs_0_, f32[256,384]{1,0:T(8,128)S(1)} %get-tuple-element.10.refs_1_, f32[144,256]{1,0:T(8,128)S(1)} %get-tuple-element.11.refs_2_), custom_call_target="tpu_custom_call" | custom-call | tf_op jit(solution)/shard_map/store_results/pallas_call | solution.py:616
